TPU v7x, 32 devices: a whole 2x2x4 slice. The times are simulated.
32 devices in a mesh: row: 16 (over z, y, core), col: 2 (over x).
Axes of the slice: x: 2, y: 2, z: 4, core: 2. Of those that a mesh axis runs over, the one named last changes fastest.
Arguments:
- pair: bfloat16 [256, 256, 128], P('row', 'col'), may hold values from -6 to 6
- relpos: bfloat16 [128, 128], replicated, may hold values from -4 to 4
- pair_gain: float32 [128], replicated, may hold values from 0.1 to 1.9
- bias_weight: bfloat16 [128, 12], replicated, may hold values from -0.5 to 0.5
- single: float32 [256, 384], P(('row', 'col')), may hold values from -6 to 6
- rotation_params: float32 [3, 256], P(None, ('row', 'col')), may hold values from -4 to 4
- translation: float32 [3, 256], P(None, ('row', 'col')), may hold values from -9 to 9
- residue_index: int32 [256], P(('row', 'col')), may hold values from 0 to 50944, as said below
- residue_mask: int32 [256], P(('row', 'col')), may hold values 0 or 1
- w_scalar: float32 [384, 576], replicated, may hold values from -0.3125 to 0.3125
- w_points: float32 [384, 576], replicated, may hold values from -0.3125 to 0.3125
- head_weights: float32 [12], replicated, may hold values from -2 to 1.5
- w_out: float32 [2112, 384], replicated, may hold values from -0.125 to 0.125
- w_hidden: float32 [384, 384], replicated, may hold values from -0.3125 to 0.3125
- w_back: float32 [384, 384], replicated, may hold values from -0.3125 to 0.3125
- w_frame: float32 [384, 6], replicated, may hold values from -0.078125 to 0.078125
Outputs:
- single_out: float32 [256, 384], P(('row', 'col'))
- frames: float32 [12, 256], P(None, ('row', 'col'))
Inputs may be any that keep to these rules, and one draw needn't show every extreme that they name: residue_index is strictly increasing along the crop, begins at 0 and ends at exactly 50944.
All inputs are finite; a program needn't handle non-finite values. No bound on the sum of `residue_mask` on one device may be relied on, other than what follows from the above.
Results may differ from a plain program's by a relative error of at most 0.0025.
Values may be sent and summed in bfloat16 or wider, within the bound.
A program may use at most 64 MiB of HBM per device.

v0:
```python
import math
import jax
import jax.numpy as jnp
from jax import lax
from jax.sharding import PartitionSpec as P

H = 12
C = 16
PQ = 4
PV = 8
BINS = 128
ITERS = 3
NORM_EPSILON = 1e-05
MASKED_LOGIT = -100000.0
NORM_FLOOR = 0.1
HIGHEST_PRECISION = lax.Precision.HIGHEST


def broadcast(value, axis, root):
    mine = lax.axis_index(axis) == root
    return lax.psum(jnp.where(mine, value, jnp.zeros_like(value)), axis)


def joined(part, axis, combine):
    gathered = jax.tree.map(lambda a: lax.all_gather(a, axis), part)

    def take(source):
        return jax.tree.map(lambda a: lax.dynamic_index_in_dim(a, source, 0, False), gathered)

    return lax.fori_loop(
        1, lax.axis_size(axis), lambda source, state: combine(state, take(source)), take(0)
    )


def layer_norm(values):
    center = values - jnp.mean(values, axis=-1, keepdims=True)
    spread = jnp.mean(center * center, axis=-1, keepdims=True)
    return center * lax.rsqrt(spread + NORM_EPSILON)


def rotation_from(update):
    quat_b, quat_c, quat_d = (update[0], update[1], update[2])
    inverse = 1.0 / (1.0 + quat_b * quat_b + quat_c * quat_c + quat_d * quat_d)
    entries = [
        1.0 + quat_b * quat_b - quat_c * quat_c - quat_d * quat_d,
        2.0 * (quat_b * quat_c - quat_d),
        2.0 * (quat_b * quat_d + quat_c),
        2.0 * (quat_b * quat_c + quat_d),
        1.0 - quat_b * quat_b + quat_c * quat_c - quat_d * quat_d,
        2.0 * (quat_c * quat_d - quat_b),
        2.0 * (quat_b * quat_d - quat_c),
        2.0 * (quat_c * quat_d + quat_b),
        1.0 - quat_b * quat_b - quat_c * quat_c + quat_d * quat_d,
    ]
    return jnp.stack(entries) * inverse


def to_global(rotation, points, translation):
    return jnp.stack(
        [
            rotation[3 * component] * points[0]
            + rotation[3 * component + 1] * points[1]
            + rotation[3 * component + 2] * points[2]
            + translation[component]
            for component in range(3)
        ]
    )


def to_local(rotation, points, translation):
    moved = [points[component] - translation[component] for component in range(3)]
    return jnp.stack(
        [
            rotation[component] * moved[0]
            + rotation[3 + component] * moved[1]
            + rotation[6 + component] * moved[2]
            for component in range(3)
        ]
    )


def compose(rotation, translation, update):
    turn = rotation_from(update[:3])
    new_rotation = jnp.stack(
        [
            rotation[3 * left] * turn[right]
            + rotation[3 * left + 1] * turn[3 + right]
            + rotation[3 * left + 2] * turn[6 + right]
            for left in range(3)
            for right in range(3)
        ]
    )
    new_translation = jnp.stack(
        [
            rotation[3 * left] * update[3]
            + rotation[3 * left + 1] * update[4]
            + rotation[3 * left + 2] * update[5]
            + translation[left]
            for left in range(3)
        ]
    )
    return (new_rotation, new_translation)


def project(single, rotation, translation, w_scalar, w_points):
    count = single.shape[0]
    scalars = jnp.dot(
        single, w_scalar, precision=HIGHEST_PRECISION, preferred_element_type=jnp.float32
    ).T
    scalars = scalars.reshape(3, H * C, count).astype(jnp.bfloat16)
    points = jnp.dot(
        single, w_points, precision=HIGHEST_PRECISION, preferred_element_type=jnp.float32
    ).T
    query_local = points[: 3 * H * PQ].reshape(3, H * PQ, count)
    key_local = points[3 * H * PQ : 6 * H * PQ].reshape(3, H * PQ, count)
    value_local = points[6 * H * PQ :].reshape(3, H * PV, count)
    return (
        scalars,
        to_global(rotation, query_local, translation),
        to_global(rotation, key_local, translation),
        to_global(rotation, value_local, translation),
    )


def advance(
    single, rotation, translation, scalar_out, point_out, pair_out, w_out, w_hidden, w_back, w_frame
):
    count = single.shape[0]
    local = to_local(rotation, point_out, translation)
    lengths = jnp.sqrt(jnp.sum(local * local, axis=0) + NORM_FLOOR)
    features = jnp.concatenate(
        [scalar_out, local.reshape(3 * H * PV, count), lengths, pair_out], axis=0
    )
    mixed = jnp.dot(
        features.T, w_out, precision=HIGHEST_PRECISION, preferred_element_type=jnp.float32
    )
    single = layer_norm(single + mixed)
    hidden = jax.nn.relu(
        jnp.dot(single, w_hidden, precision=HIGHEST_PRECISION, preferred_element_type=jnp.float32)
    )
    single = layer_norm(
        single
        + jnp.dot(hidden, w_back, precision=HIGHEST_PRECISION, preferred_element_type=jnp.float32)
    )
    update = jnp.dot(
        single, w_frame, precision=HIGHEST_PRECISION, preferred_element_type=jnp.float32
    ).T
    rotation, translation = compose(rotation, translation, update)
    return (single, rotation, translation)


def attend_block(
    query, keyval, query_side, key_side, value_side, bias, normed, pair_live, point_scale
):
    heads_query = query.reshape(H, C, -1)
    keys = keyval[0].reshape(H, C, -1)
    values = keyval[1].reshape(H, C, -1)
    query_grid = query_side.reshape(3, H, PQ, -1)
    key_grid = key_side.reshape(3, H, PQ, -1)
    value_grid = value_side.reshape(3, H, PV, -1)
    scores = jnp.einsum(
        "hci,hcj->hij", heads_query, keys, preferred_element_type=jnp.float32
    ) / math.sqrt(C)
    cross = jnp.einsum("ahpi,ahpj->hij", query_grid, key_grid, precision=HIGHEST_PRECISION)
    distance = (
        jnp.sum(query_grid * query_grid, axis=(0, 2))[:, :, None]
        + jnp.sum(key_grid * key_grid, axis=(0, 2))[:, None, :]
        - 2.0 * cross
    )
    logits = math.sqrt(1.0 / 3.0) * (scores + bias - point_scale[:, None, None] * distance)
    logits = jnp.where(pair_live[None], logits, MASKED_LOGIT)
    local_max = jnp.max(logits, axis=-1)
    unscaled = jnp.exp(logits - local_max[:, :, None])
    total_weight = jnp.sum(unscaled, axis=-1)
    rounded = unscaled.astype(jnp.bfloat16)
    scalar_sum = jnp.einsum("hij,hcj->hci", rounded, values, preferred_element_type=jnp.float32)
    point_sum = jnp.einsum("hij,ahpj->ahpi", unscaled, value_grid, precision=HIGHEST_PRECISION)
    pair_sum = jnp.einsum("hij,ijc->hci", rounded, normed, preferred_element_type=jnp.float32)
    return (local_max, total_weight, scalar_sum, point_sum, pair_sum)


def merge_softmax(first, second):
    top = jnp.maximum(first[0], second[0])
    lead = jnp.exp(first[0] - top)
    trail = jnp.exp(second[0] - top)
    return (
        top,
        first[1] * lead + second[1] * trail,
        first[2] * lead[:, None, :] + second[2] * trail[:, None, :],
        first[3] * lead[None, :, None, :] + second[3] * trail[None, :, None, :],
        first[4] * lead[:, None, :] + second[4] * trail[:, None, :],
    )


def body(
    pair,
    relpos,
    pair_gain,
    bias_weight,
    single,
    rotation_params,
    translation,
    residue_index,
    residue_mask,
    w_scalar,
    w_points,
    head_weights,
    w_out,
    w_hidden,
    w_back,
    w_frame,
):
    row_rows = pair.shape[0]
    col_rows = pair.shape[1]
    owned = single.shape[0]
    row_place = lax.axis_index("row")
    col_place = lax.axis_index("col")
    index_all, mask_all = (
        lax.all_gather(residue_index, ("row", "col"), axis=0, tiled=True),
        lax.all_gather(residue_mask, ("row", "col"), axis=0, tiled=True),
    )
    query_index = lax.dynamic_slice_in_dim(index_all, row_place * row_rows, row_rows, 0)
    key_index = lax.dynamic_slice_in_dim(index_all, col_place * col_rows, col_rows, 0)
    query_live = lax.dynamic_slice_in_dim(mask_all, row_place * row_rows, row_rows, 0) == 1
    key_live = lax.dynamic_slice_in_dim(mask_all, col_place * col_rows, col_rows, 0) == 1
    pair_live = query_live[:, None] & key_live[None, :]
    span_rows = math.gcd(row_rows, 64)

    def prepare(index):
        offset = (
            jnp.clip(key_index[None, :] - query_index[:, None], -(BINS // 2), BINS // 2 - 1)
            + BINS // 2
        )
        onehot = (offset[:, :, None] == lax.broadcasted_iota(jnp.int32, (1, 1, BINS), 2)).astype(
            jnp.bfloat16
        )
        embedded = jnp.dot(
            onehot.reshape(span_rows * col_rows, BINS), relpos, preferred_element_type=jnp.float32
        )
        summed = pair.astype(jnp.float32) + embedded.reshape(span_rows, col_rows, -1)
        normed_part = (layer_norm(summed) * pair_gain).astype(jnp.bfloat16)
        bias_part = jnp.einsum(
            "ijc,ch->hij", normed_part, bias_weight, preferred_element_type=jnp.float32
        )
        return (normed_part, bias_part)

    normed_blocks, bias_blocks = lax.map(
        prepare, jnp.arange(row_rows // span_rows, dtype=jnp.int32)
    )
    normed = normed_blocks.reshape(row_rows, col_rows, -1)
    bias = bias_blocks.transpose(1, 0, 2, 3).reshape(H, row_rows, col_rows)
    point_scale = jax.nn.softplus(head_weights) * (math.sqrt(2.0 / (9.0 * PQ)) / 2.0)
    rotation = rotation_from(rotation_params)
    state = single
    for step in range(ITERS):
        scalars, query_points, key_points, value_points = project(
            state, rotation, translation, w_scalar, w_points
        )
        query_flat = query_points.reshape(-1, owned)
        key_flat = key_points.reshape(-1, owned)
        value_flat = value_points.reshape(-1, owned)
        block_scalar = lax.all_gather(scalars, "col", axis=2, tiled=True)
        block_point = (
            lax.all_gather(query_flat, "col", axis=1, tiled=True),
            lax.all_gather(key_flat, "col", axis=1, tiled=True),
            lax.all_gather(value_flat, "col", axis=1, tiled=True),
        )
        query = block_scalar[0]
        query_side = block_point[0]
        ratio = lax.axis_size("row") // lax.axis_size("col")
        scalar_pieces = []
        key_pieces = []
        value_pieces = []
        for part in range(ratio):
            root = col_place * ratio + part
            scalar_pieces.append(broadcast(block_scalar[1:], "row", root))
            key_piece, value_piece = (
                broadcast(block_point[1], "row", root),
                broadcast(block_point[2], "row", root),
            )
            key_pieces.append(key_piece)
            value_pieces.append(value_piece)
        keyval = jnp.concatenate(scalar_pieces, axis=2)
        key_side = jnp.concatenate(key_pieces, axis=1)
        value_side = jnp.concatenate(value_pieces, axis=1)
        local_max, total_weight, scalar_sum, point_sum, pair_sum = attend_block(
            query, keyval, query_side, key_side, value_side, bias, normed, pair_live, point_scale
        )
        pair_out = None
        merged = joined(
            (local_max, total_weight, scalar_sum, point_sum, pair_sum), "col", merge_softmax
        )
        begin = col_place * owned
        total = lax.dynamic_slice_in_dim(merged[1], begin, owned, 1)
        scalar_share = lax.dynamic_slice_in_dim(merged[2], begin, owned, 2)
        point_share = lax.dynamic_slice_in_dim(merged[3], begin, owned, 3)
        pair_share = lax.dynamic_slice_in_dim(merged[4], begin, owned, 2)
        scalar_out = (scalar_share / total[:, None, :]).reshape(H * C, owned)
        point_out = (point_share / total[None, :, None, :]).reshape(3, H * PV, owned)
        pair_out = (pair_share / total[:, None, :]).reshape(-1, owned)
        state, rotation, translation = advance(
            state,
            rotation,
            translation,
            scalar_out,
            point_out,
            pair_out,
            w_out,
            w_hidden,
            w_back,
            w_frame,
        )
    frames = jnp.concatenate([rotation, translation], axis=0)
    return (state, frames)


def solution(mesh):
    placed = (
        P("row", "col", None),
        P(),
        P(),
        P(),
        P(("row", "col"), None),
        P(None, ("row", "col")),
        P(None, ("row", "col")),
        P(("row", "col")),
        P(("row", "col")),
        P(),
        P(),
        P(),
        P(),
        P(),
        P(),
        P(),
    )
    return jax.shard_map(
        body,
        mesh=mesh,
        in_specs=placed,
        out_specs=(P(("row", "col"), None), P(None, ("row", "col"))),
        check_vma=False,
    )
```

profile of v0, /device:TPU:8, one launch (start us, length us, event | category | flops | bytes accessed | tf_op | source)
XLA Modules:
  0.0 855.9 jit_solution(17176998492599648123)
XLA Ops:
  7.3 2.2 convolution_convert_fusion.2
  9.6 4.4 all_gather.132
  17.3 2.0 fusion.125
  19.9 4.4 all_gather.143
  24.4 4.3 all_gather.136
  30.7 40.5 %all-reduce.2 = (s32[256]{0:T(256)S(1)}, s32[256]{0:T(256)S(1)}) all-reduce(s32[256]{0:T(256)S(1)} %dynamic-update-slice.1, s32[256]{0:T(256)S(1)} %dynamic-update-slice), channel_id=1, replica_groups=mesh['row'=16,'col'=2] {'row','col'}, use_global_device_ids=true, to_apply=%add.1 | all-reduce | flops 512 | bytes 4096
  72.2 4.6 all_gather.135
  78.2 2.1 copy.358
  80.4 1.8 fusion.115
  83.4 1.5 multiply_convert_fusion
  85.9 22.8 %all-reduce.26.cloned.1.call-done = (bf16[2,192,16]{1,2,0:T(8,128)(2,1)}, bf16[2,192,16]{1,2,0:T(8,128)(2,1)}, bf16[2,192,16]{1,2,0:T(8,128)(2,1)}, bf16[2,192,1...) async-done(((bf16[2,192,16]{1,2,0:T(8,128)(2,1)}, ...) | async-done | bytes 98320 | tf_op jit(solution)/shard_map/psum | solution.py:21
  115.1 1.6 copy.356
  117.3 90.8 %all-reduce.20.cloned.1.call-done = (f32[144,16]{0,1:T(8,128)}, f32[144,16]{0,1:T(8,128)}, f32[144,16]{0,1:T(8,128)}, f32[144,16]{0,1:T(8,128)}, f32[144,16]{0,1...) async-done(((f32[144,16]{0,1:T(8,128)}, f32[144,16]{0,1:T(8,128)}, ...) | async-done | bytes 221200 | tf_op jit(solution)/shard_map/psum | solution.py:21
  221.1 1.3 constant_dynamic-update-slice_fusion.22
  227.8 1.4 constant_dynamic-update-slice_fusion.17
  230.5 1.7 copy.368
  234.5 1.3 convolution_bitcast_fusion.2
  235.9 4.4 all-gather.15
  240.3 4.4 all-gather.16
  244.6 1.4 convolution_bitcast_fusion.5
  247.1 6.0 all-gather.4
  253.7 5.4 all-gather
  260.0 1.6 copy.425
  261.5 5.8 all-gather.3
  271.0 2.5 fusion.117
  275.5 2.0 fusion.21
  277.5 2.0 convolution_bitcast_fusion.10
  280.1 4.4 all_gather.148
  284.8 4.3 all_gather.149
  289.2 4.3 all_gather.150
  293.5 4.4 all_gather.157
  301.1 91.5 %all-reduce.24.cloned.1.call-done = (bf16[2,192,16]{1,2,0:T(8,128)(2,1)}, bf16[2,192,16]{1,2,0:T(8,128)(2,1)}, bf16[2,192,16]{1,2,0:T(8,128)(2,1)}, bf16[2,192,1...) async-done(((bf16[2,192,16]{1,2,0:T(8,128)(2,1)}, ...) | async-done | bytes 98320 | tf_op jit(solution)/shard_map/psum | solution.py:21
  399.1 1.6 copy.379
  401.3 90.7 %all-reduce.18.cloned.1.call-done = (f32[144,16]{0,1:T(8,128)}, f32[144,16]{0,1:T(8,128)}, f32[144,16]{0,1:T(8,128)}, f32[144,16]{0,1:T(8,128)}, f32[144,16]{0,1...) async-done(((f32[144,16]{0,1:T(8,128)}, f32[144,16]{0,1:T(8,128)}, ...) | async-done | bytes 221200 | tf_op jit(solution)/shard_map/psum | solution.py:21
  505.8 4.4 all-gather.17
  510.4 4.4 all-gather.18
  514.7 1.4 convolution_bitcast_fusion.4
  517.2 6.0 all-gather.9
  523.8 5.3 all-gather.5
  529.9 1.6 copy.429
  532.8 1.3 constant_dynamic-update-slice_fusion.46
  539.6 1.4 constant_dynamic-update-slice_fusion.41
  542.3 1.7 copy.387
  543.9 1.3 convolution_bitcast_fusion.1
  545.3 5.8 all-gather.8
  554.8 2.5 fusion.120
  563.2 2.0 fusion.22
  565.2 2.0 convolution_bitcast_fusion.9
  567.8 4.4 all_gather.162
  572.5 4.3 all_gather.163
  576.9 4.3 all_gather.164
  581.2 4.4 all_gather.171
  588.6 91.3 %all-reduce.22.cloned.1.call-done = (bf16[2,192,16]{1,2,0:T(8,128)(2,1)}, bf16[2,192,16]{1,2,0:T(8,128)(2,1)}, bf16[2,192,16]{1,2,0:T(8,128)(2,1)}, bf16[2,192,1...) async-done(((bf16[2,192,16]{1,2,0:T(8,128)(2,1)}, ...) | async-done | bytes 98320 | tf_op jit(solution)/shard_map/psum | solution.py:21
  686.3 1.6 copy.398
  688.6 90.7 %all-reduce.16.cloned.1.call-done = (f32[144,16]{0,1:T(8,128)}, f32[144,16]{0,1:T(8,128)}, f32[144,16]{0,1:T(8,128)}, f32[144,16]{0,1:T(8,128)}, f32[144,16]{0,1...) async-done(((f32[144,16]{0,1:T(8,128)}, f32[144,16]{0,1:T(8,128)}, ...) | async-done | bytes 221200 | tf_op jit(solution)/shard_map/psum | solution.py:21
  793.1 4.4 all-gather.19
  797.6 1.4 convolution_bitcast_fusion.3
  799.1 4.4 all-gather.20
  804.4 5.3 all-gather.10
  811.5 5.3 all-gather.14
  828.1 1.7 copy.406
  829.8 1.3 convolution_bitcast_fusion
  831.2 6.0 all-gather.13
  840.2 2.5 fusion.123
  (446 shorter events, 140.5 us)
Async XLA Ops:
  7.2 263.8 %copy-start = (f32[2112,384]{1,0:T(8,128)S(1)}, f32[2112,384]{1,0:T(8,128)}, u32[]{:S(2)}) copy-start(f32[2112,384]{1,0:T(8,128)} %param.28) | copy-start | bytes 9732100
  7.2 23.0 %copy-start.66 = (s32[8]{0:T(128)S(1)}, s32[8]{0:T(128)}, u32[]{:S(2)}) copy-start(s32[8]{0:T(128)} %param.23) | copy-start | bytes 100
  7.2 23.3 %copy-start.67 = (s32[8]{0:T(128)S(1)}, s32[8]{0:T(128)}, u32[]{:S(2)}) copy-start(s32[8]{0:T(128)} %param.24) | copy-start | bytes 100
  7.2 64.3 %copy-start.68 = (f32[12]{0:T(128)S(1)}, f32[12]{0:T(128)}, u32[]{:S(2)}) copy-start(f32[12]{0:T(128)} %param.27) | copy-start | bytes 148
  7.2 73.2 %copy-start.13 = (bf16[128,128]{1,0:T(8,128)(2,1)S(1)}, bf16[128,128]{1,0:T(8,128)(2,1)}, u32[]{:S(2)}) copy-start(bf16[128,128]{1,0:T(8,128)(2,1)} %param.17) | copy-start | bytes 98308
  7.2 101.5 %all-reduce.26.cloned.1.call-start = ((), (), s32[]{:S(2)}) async-start(), calls=%async_computation.5 | async-start | bytes 262144 | tf_op jit(solution)/shard_map/psum | solution.py:21
  14.6 68.8 %copy-start.65 = (f32[128]{0:T(128)S(1)}, f32[128]{0:T(128)}, u32[]{:S(2)}) copy-start(f32[128]{0:T(128)} %param.18) | copy-start | bytes 1540
  14.7 193.5 %all-reduce.20.cloned.1.call-start = ((), (), s32[]{:S(2)}) async-start(), calls=%async_computation.2 | async-start | bytes 655360 | tf_op jit(solution)/shard_map/psum | solution.py:21
  17.1 7.2 copy-start.55
  17.1 7.2 copy-start.56
  17.1 7.2 copy-start.57
  17.3 7.0 copy-start.54
  28.8 56.9 %copy-start.64 = (bf16[128,12]{0,1:T(8,128)(2,1)S(1)}, bf16[128,12]{0,1:T(8,128)(2,1)}, u32[]{:S(2)}) copy-start(bf16[128,12]{0,1:T(8,128)(2,1)} %param.19) | copy-start | bytes 9220
  30.1 362.5 %all-reduce.24.cloned.1.call-start = ((), (), s32[]{:S(2)}) async-start(), calls=%async_computation.4 | async-start | bytes 262144 | tf_op jit(solution)/shard_map/psum | solution.py:21
  80.4 151.8 %copy-start.60 = (f32[12]{0:T(128)S(1)}, f32[12]{0:T(128)}, u32[]{:S(2)}) copy-start(f32[12]{0:T(128)} %fusion.102) | copy-start | bytes 148
  83.4 152.5 %copy-start.11 = (pred[16,128]{1,0:T(8,128)(4,1)}, pred[16,128]{1,0:T(8,128)(4,1)S(1)}, u32[]{:S(2)}) copy-start(pred[16,128]{1,0:T(8,128)(4,1)S(1)} %broadcast_and_fusion) | copy-start | bytes 6148
  268.2 6.8 copy-start.44
  271.0 2.8 copy-start.3
  271.0 3.2 copy-start.6
  271.0 4.2 copy-start.61
  274.8 4.7 copy-start.59
  275.0 4.8 copy-start.63
  275.2 9.3 %copy-start.39 = (f32[1,8]{1,0:T(1,128)}, f32[1,8]{1,0:T(1,128)S(1)}, u32[]{:S(2)}) copy-start(f32[1,8]{1,0:T(1,128)S(1)} %get-tuple-element.382) | copy-start | bytes 100
  275.2 9.4 %copy-start.40 = (f32[1,8]{1,0:T(1,128)}, f32[1,8]{1,0:T(1,128)S(1)}, u32[]{:S(2)}) copy-start(f32[1,8]{1,0:T(1,128)S(1)} %get-tuple-element.381) | copy-start | bytes 100
  275.3 9.2 %copy-start.38 = (f32[1,8]{1,0:T(1,128)}, f32[1,8]{1,0:T(1,128)S(1)}, u32[]{:S(2)}) copy-start(f32[1,8]{1,0:T(1,128)S(1)} %get-tuple-element.468) | copy-start | bytes 100
  275.4 4.6 copy-start.34
  275.4 9.1 %copy-start.37 = (f32[1,8]{1,0:T(1,128)}, f32[1,8]{1,0:T(1,128)S(1)}, u32[]{:S(2)}) copy-start(f32[1,8]{1,0:T(1,128)S(1)} %get-tuple-element.361) | copy-start | bytes 100
  275.4 9.1 %copy-start.36 = (f32[1,8]{1,0:T(1,128)}, f32[1,8]{1,0:T(1,128)S(1)}, u32[]{:S(2)}) copy-start(f32[1,8]{1,0:T(1,128)S(1)} %get-tuple-element.360) | copy-start | bytes 100
  275.4 4.5 copy-start.24
  275.4 4.5 copy-start.25
  275.4 4.6 copy-start.35
  275.5 4.4 copy-start.16
  275.5 4.4 copy-start.17
  275.5 9.3 %copy-start.14 = (f32[1,8]{1,0:T(1,128)}, f32[1,8]{1,0:T(1,128)S(1)}, u32[]{:S(2)}) copy-start(f32[1,8]{1,0:T(1,128)S(1)} %get-tuple-element.364) | copy-start | bytes 100
  300.0 192.0 %all-reduce.18.cloned.1.call-start = ((), (), s32[]{:S(2)}) async-start(), calls=%async_computation.1 | async-start | bytes 655360 | tf_op jit(solution)/shard_map/psum | solution.py:21
  301.1 378.8 %all-reduce.22.cloned.1.call-start = ((), (), s32[]{:S(2)}) async-start(), calls=%async_computation.3 | async-start | bytes 262144 | tf_op jit(solution)/shard_map/psum | solution.py:21
  505.8 46.3 %copy-start.15 = (f32[1,8]{1,0:T(1,128)S(1)}, f32[1,8]{1,0:T(1,128)}, u32[]{:S(2)}) copy-start(f32[1,8]{1,0:T(1,128)} %copy-done.14) | copy-start | bytes 100
  529.2 22.0 %copy-start.9 = (f32[12,8]{1,0:T(8,128)}, f32[12,8]{1,0:T(8,128)S(1)}, u32[]{:S(2)}) copy-start(f32[12,8]{1,0:T(8,128)S(1)} %get-tuple-element.421) | copy-start | bytes 1156
  552.0 6.7 copy-start.45
  554.8 2.7 copy-start.4
  554.8 3.2 copy-start.7
  558.0 234.0 %copy-start.12 = (pred[16,128]{1,0:T(8,128)(4,1)S(1)}, pred[16,128]{1,0:T(8,128)(4,1)}, u32[]{:S(2)}) copy-start(pred[16,128]{1,0:T(8,128)(4,1)} %copy-done.11) | copy-start | bytes 6148
  558.5 13.7 %copy-start.58 = (f32[8]{0:T(128)}, f32[8]{0:T(128)S(1)}, u32[]{:S(2)}) copy-start(f32[8]{0:T(128)S(1)} %broadcast_multiply_fusion.7) | copy-start | bytes 100
  558.7 8.5 copy-start.62
  559.6 7.8 copy-start.41
  560.3 11.9 %copy-start.42 = (f32[1,8]{1,0:T(1,128)}, f32[1,8]{1,0:T(1,128)S(1)}, u32[]{:S(2)}) copy-start(f32[1,8]{1,0:T(1,128)S(1)} %get-tuple-element.447) | copy-start | bytes 100
  561.0 11.2 %copy-start.43 = (f32[1,8]{1,0:T(1,128)}, f32[1,8]{1,0:T(1,128)S(1)}, u32[]{:S(2)}) copy-start(f32[1,8]{1,0:T(1,128)S(1)} %get-tuple-element.452) | copy-start | bytes 100
  561.8 5.8 copy-start.18
  561.8 5.8 copy-start.20
  561.8 10.6 %copy-start.22 = (f32[1,8]{1,0:T(1,128)}, f32[1,8]{1,0:T(1,128)S(1)}, u32[]{:S(2)}) copy-start(f32[1,8]{1,0:T(1,128)S(1)} %get-tuple-element.409) | copy-start | bytes 100
  562.5 9.9 %copy-start.26 = (f32[1,8]{1,0:T(1,128)}, f32[1,8]{1,0:T(1,128)S(1)}, u32[]{:S(2)}) copy-start(f32[1,8]{1,0:T(1,128)S(1)} %get-tuple-element.410) | copy-start | bytes 100
  562.5 9.9 %copy-start.28 = (f32[1,8]{1,0:T(1,128)}, f32[1,8]{1,0:T(1,128)S(1)}, u32[]{:S(2)}) copy-start(f32[1,8]{1,0:T(1,128)S(1)} %get-tuple-element.411) | copy-start | bytes 100
  562.5 9.9 %copy-start.30 = (f32[1,8]{1,0:T(1,128)}, f32[1,8]{1,0:T(1,128)S(1)}, u32[]{:S(2)}) copy-start(f32[1,8]{1,0:T(1,128)S(1)} %get-tuple-element.412) | copy-start | bytes 100
  563.2 4.5 copy-start.31
  563.2 4.5 copy-start.32
  563.2 9.0 %copy-start.33 = (f32[1,8]{1,0:T(1,128)}, f32[1,8]{1,0:T(1,128)S(1)}, u32[]{:S(2)}) copy-start(f32[1,8]{1,0:T(1,128)S(1)} %get-tuple-element.415) | copy-start | bytes 100
  587.7 191.6 %all-reduce.16.cloned.1.call-start = ((), (), s32[]{:S(2)}) async-start(), calls=%async_computation | async-start | bytes 655360 | tf_op jit(solution)/shard_map/psum | solution.py:21
  793.0 45.2 %copy-start.19 = (f32[1,8]{1,0:T(1,128)S(1)}, f32[1,8]{1,0:T(1,128)}, u32[]{:S(2)}) copy-start(f32[1,8]{1,0:T(1,128)} %copy-done.18) | copy-start | bytes 100
  793.0 45.2 %copy-start.21 = (f32[1,8]{1,0:T(1,128)S(1)}, f32[1,8]{1,0:T(1,128)}, u32[]{:S(2)}) copy-start(f32[1,8]{1,0:T(1,128)} %copy-done.20) | copy-start | bytes 100
  793.1 45.2 %copy-start.23 = (f32[1,8]{1,0:T(1,128)S(1)}, f32[1,8]{1,0:T(1,128)}, u32[]{:S(2)}) copy-start(f32[1,8]{1,0:T(1,128)} %copy-done.22) | copy-start | bytes 100
  837.2 8.4 copy-start.27
  837.2 8.4 copy-start.29
  840.2 3.2 copy-start.8
  844.2 4.9 copy-start.10
  (11 other events, 24.6 us)
Sparse Core Ops, SparseCore 0:
  14.8 93.8 all-reduce.25
  113.9 94.2 all-reduce.19
  300.2 92.4 all-reduce.23
  397.7 94.3 all-reduce.17
  587.9 91.9 all-reduce.21
  685.0 94.3 all-reduce.15
where the time goes:
time: 862 us; the launch traced here: 856 us
  waiting for transfers between devices  478 us (55%)
  blocking collectives  170 us (20%)
  local copies, waits for them, and re-layouts  119 us (14%)
  matrix products  43.3 us (5%)
  other arithmetic  29.7 us (3%)
  between operations  15.7 us (2%)
    psum x6, waiting for transfers between devices, broadcast(): return lax.psum(jnp.where(mine, value, jnp.zeros_like(value)), axis)  478 us
    all_gather x15, blocking collectives, joined(): gathered = jax.tree.map(lambda a: lax.all_gather(a, axis), part)  77 us
    unnamed x207, local copies, waits for them, and re-layouts  76.3 us
    unnamed x1, blocking collectives  40.5 us
  transfers between devices with their start and end apart: 6, of which 6 were waited for; matrix products, arithmetic and copies ran while one was open for 5% of the time, Pallas kernels for 0%

commit v1 on v0

--- a/solution.py
+++ b/solution.py
@@ -18,7 +18,11 @@
 
 def broadcast(value, axis, root):
     mine = lax.axis_index(axis) == root
-    return lax.psum(jnp.where(mine, value, jnp.zeros_like(value)), axis)
+
+    def load_the_packet(incoming_x, peer_axis):
+        return jax.lax.all_gather(incoming_x, peer_axis).sum(axis=0)
+
+    return load_the_packet(jnp.where(mine, value, jnp.zeros_like(value)), axis)
 
 
 def joined(part, axis, combine):

time: 862 us -> 1920 us (2.23)
  blocking collectives: 170 us -> 1620 us
  waiting for transfers between devices: 478 us -> 0 us
  other arithmetic: 29.7 us -> 116 us
    all_gather x0 -> x72, blocking collectives: none -> 1450 us  [load_the_packet(): return jax.lax.all_gather(incoming_x, peer_axis).sum(axis=0)]
    psum x6 -> x0, waiting for transfers between devices: 478 us -> none  [broadcast(): return lax.psum(jnp.where(mine, value, jnp.zeros_like(value)), axis)]
    reduce_sum x0 -> x72, other arithmetic: none -> 79.8 us  [load_the_packet(): return jax.lax.all_gather(incoming_x, peer_axis).sum(axis=0)]
    unnamed x207 -> x259, local copies, waits for them, and re-layouts: 76.3 us -> 69.6 us
  transfers between devices with their start and end apart: 6 -> 0, of which waited for: 6 -> 0; matrix products, arithmetic and copies ran while one was open for 5% -> 0% of each run, Pallas kernels for 0% -> 0%
where the time goes in v1:
time: 1920 us; the launch traced here: 1900 us
  blocking collectives  1620 us (84%)
  local copies, waits for them, and re-layouts  116 us (6%)
  other arithmetic  116 us (6%)
  matrix products  44.2 us (2%)
    all_gather x72, blocking collectives, load_the_packet(): return jax.lax.all_gather(incoming_x, peer_axis).sum(axis=0)  1450 us
    reduce_sum x72, other arithmetic, load_the_packet(): return jax.lax.all_gather(incoming_x, peer_axis).sum(axis=0)  79.8 us
    all_gather x15, blocking collectives, joined(): gathered = jax.tree.map(lambda a: lax.all_gather(a, axis), part)  79.3 us
    unnamed x259, local copies, waits for them, and re-layouts  69.6 us
    unnamed x1, blocking collectives  41.9 us

profile of v1, /device:TPU:8, one launch (start us, length us, event | category | flops | bytes accessed | tf_op | source)
XLA Modules:
  0.0 1900.4 jit_solution(11338362409022594309)
XLA Ops:
  11.9 19.5 %all-gather.87 = f32[16,144,16]{1,2,0:T(8,128)S(1)} all-gather(f32[1,144,16]{1,2,0:T(8,128)S(1)} %get-tuple-element.308), channel_id=10, replica_groups=mesh['row'=16,'col'=2] {'row'}, dimensions={0}, use_global_device_ids=true | all-gather | bytes 156672 | tf_op jit(solution)/shard_map/all_gather | solution.py:23
  53.7 19.7 %all-gather.89 = f32[16,144,16]{1,2,0:T(8,128)S(1)} all-gather(f32[1,144,16]{1,2,0:T(8,128)} %get-tuple-element.306), channel_id=12, replica_groups=mesh['row'=16,'col'=2] {'row'}, dimensions={0}, use_global_device_ids=true | all-gather | bytes 156672 | tf_op jit(solution)/shard_map/all_gather | solution.py:23
  95.7 19.7 %all-gather.91 = f32[16,144,16]{1,2,0:T(8,128)S(1)} all-gather(f32[1,144,16]{1,2,0:T(8,128)} %get-tuple-element.304), channel_id=14, replica_groups=mesh['row'=16,'col'=2] {'row'}, dimensions={0}, use_global_device_ids=true | all-gather | bytes 156672 | tf_op jit(solution)/shard_map/all_gather | solution.py:23
  137.6 19.7 %all-gather.93 = f32[16,144,16]{1,2,0:T(8,128)S(1)} all-gather(f32[1,144,16]{1,2,0:T(8,128)} %get-tuple-element.302), channel_id=16, replica_groups=mesh['row'=16,'col'=2] {'row'}, dimensions={0}, use_global_device_ids=true | all-gather | bytes 156672 | tf_op jit(solution)/shard_map/all_gather | solution.py:23
  193.2 19.4 %all-gather = bf16[32,192,16]{1,2,0:T(8,128)(2,1)S(1)} all-gather(bf16[2,192,16]{1,2,0:T(8,128)(2,1)S(1)} %get-tuple-element.239), channel_id=2, replica_groups=mesh['row'=16,'col'=2] {'row'}, dimensions={0}, use_global_device_ids=true | all-gather | bytes 208896 | tf_op jit(solution)/shard_map/all_gather | solution.py:23
  235.0 19.7 %all-gather.2 = bf16[32,192,16]{1,2,0:T(8,128)(2,1)S(1)} all-gather(bf16[2,192,16]{1,2,0:T(8,128)(2,1)} %get-tuple-element.234), channel_id=4, replica_groups=mesh['row'=16,'col'=2] {'row'}, dimensions={0}, use_global_device_ids=true | all-gather | bytes 208896 | tf_op jit(solution)/shard_map/all_gather | solution.py:23
  277.0 19.6 %all-gather.4 = bf16[32,192,16]{1,2,0:T(8,128)(2,1)S(1)} all-gather(bf16[2,192,16]{1,2,0:T(8,128)(2,1)} %get-tuple-element.236), channel_id=6, replica_groups=mesh['row'=16,'col'=2] {'row'}, dimensions={0}, use_global_device_ids=true | all-gather | bytes 208896 | tf_op jit(solution)/shard_map/all_gather | solution.py:23
  319.1 19.6 %all-gather.6 = bf16[32,192,16]{1,2,0:T(8,128)(2,1)S(1)} all-gather(bf16[2,192,16]{1,2,0:T(8,128)(2,1)} %get-tuple-element.238), channel_id=8, replica_groups=mesh['row'=16,'col'=2] {'row'}, dimensions={0}, use_global_device_ids=true | all-gather | bytes 208896 | tf_op jit(solution)/shard_map/all_gather | solution.py:23
  364.7 41.9 %all-reduce.2 = (s32[256]{0:T(256)S(1)}, s32[256]{0:T(256)S(1)}) all-reduce(s32[256]{0:T(256)S(1)} %dynamic-update-slice.1, s32[256]{0:T(256)S(1)} %dynamic-update-slice), channel_id=1, replica_groups=mesh['row'=16,'col'=2] {'row','col'}, use_global_device_ids=true, to_apply=%add.1 | all-reduce | flops 512 | bytes 4096
  464.7 20.1 %all-gather.98 = f32[16,288,16]{1,2,0:T(8,128)} all-gather(f32[1,288,16]{1,2,0:T(8,128)} %get-tuple-element.230), channel_id=22, replica_groups=mesh['row'=16,'col'=2] {'row'}, dimensions={0}, use_global_device_ids=true | all-gather | bytes 313344 | tf_op jit(solution)/shard_map/all_gather | solution.py:23
  487.8 21.5 %all-gather.99 = f32[16,288,16]{1,2,0:T(8,128)} all-gather(f32[1,288,16]{1,2,0:T(8,128)} %get-tuple-element.229), channel_id=23, replica_groups=mesh['row'=16,'col'=2] {'row'}, dimensions={0}, use_global_device_ids=true | all-gather | bytes 313344 | tf_op jit(solution)/shard_map/all_gather | solution.py:23
  512.2 19.9 %all-gather.100 = f32[16,288,16]{1,2,0:T(8,128)} all-gather(f32[1,288,16]{1,2,0:T(8,128)S(1)} %get-tuple-element.228), channel_id=24, replica_groups=mesh['row'=16,'col'=2] {'row'}, dimensions={0}, use_global_device_ids=true | all-gather | bytes 313344 | tf_op jit(solution)/shard_map/all_gather | solution.py:23
  533.8 21.6 %all-gather.101 = f32[16,288,16]{1,2,0:T(8,128)} all-gather(f32[1,288,16]{1,2,0:T(8,128)} %get-tuple-element.227), channel_id=25, replica_groups=mesh['row'=16,'col'=2] {'row'}, dimensions={0}, use_global_device_ids=true | all-gather | bytes 313344 | tf_op jit(solution)/shard_map/all_gather | solution.py:23
  558.4 20.1 %all-gather.102 = f32[16,288,16]{1,2,0:T(8,128)} all-gather(f32[1,288,16]{1,2,0:T(8,128)} %get-tuple-element.226), channel_id=26, replica_groups=mesh['row'=16,'col'=2] {'row'}, dimensions={0}, use_global_device_ids=true | all-gather | bytes 313344 | tf_op jit(solution)/shard_map/all_gather | solution.py:23
  581.5 22.0 %all-gather.103 = f32[16,288,16]{1,2,0:T(8,128)} all-gather(f32[1,288,16]{1,2,0:T(8,128)} %get-tuple-element.225), channel_id=27, replica_groups=mesh['row'=16,'col'=2] {'row'}, dimensions={0}, use_global_device_ids=true | all-gather | bytes 313344 | tf_op jit(solution)/shard_map/all_gather | solution.py:23
  606.5 20.1 %all-gather.104 = f32[16,288,16]{1,2,0:T(8,128)} all-gather(f32[1,288,16]{1,2,0:T(8,128)} %get-tuple-element.224), channel_id=28, replica_groups=mesh['row'=16,'col'=2] {'row'}, dimensions={0}, use_global_device_ids=true | all-gather | bytes 313344 | tf_op jit(solution)/shard_map/all_gather | solution.py:23
  669.9 20.9 %all-gather.105 = f32[16,144,16]{1,2,0:T(8,128)} all-gather(f32[1,144,16]{1,2,0:T(8,128)S(1)} %get-tuple-element.287), channel_id=39, replica_groups=mesh['row'=16,'col'=2] {'row'}, dimensions={0}, use_global_device_ids=true | all-gather | bytes 156672 | tf_op jit(solution)/shard_map/all_gather | solution.py:23
  692.4 19.7 %all-gather.106 = f32[16,144,16]{1,2,0:T(8,128)} all-gather(f32[1,144,16]{1,2,0:T(8,128)S(1)} %get-tuple-element.286), channel_id=40, replica_groups=mesh['row'=16,'col'=2] {'row'}, dimensions={0}, use_global_device_ids=true | all-gather | bytes 156672 | tf_op jit(solution)/shard_map/all_gather | solution.py:23
  713.6 20.9 %all-gather.107 = f32[16,144,16]{1,2,0:T(8,128)} all-gather(f32[1,144,16]{1,2,0:T(8,128)S(1)} %get-tuple-element.285), channel_id=41, replica_groups=mesh['row'=16,'col'=2] {'row'}, dimensions={0}, use_global_device_ids=true | all-gather | bytes 156672 | tf_op jit(solution)/shard_map/all_gather | solution.py:23
  736.1 19.5 %all-gather.108 = f32[16,144,16]{1,2,0:T(8,128)} all-gather(f32[1,144,16]{1,2,0:T(8,128)S(1)} %get-tuple-element.284), channel_id=42, replica_groups=mesh['row'=16,'col'=2] {'row'}, dimensions={0}, use_global_device_ids=true | all-gather | bytes 156672 | tf_op jit(solution)/shard_map/all_gather | solution.py:23
  757.2 20.9 %all-gather.109 = f32[16,144,16]{1,2,0:T(8,128)} all-gather(f32[1,144,16]{1,2,0:T(8,128)S(1)} %get-tuple-element.283), channel_id=43, replica_groups=mesh['row'=16,'col'=2] {'row'}, dimensions={0}, use_global_device_ids=true | all-gather | bytes 156672 | tf_op jit(solution)/shard_map/all_gather | solution.py:23
  779.6 19.5 %all-gather.110 = f32[16,144,16]{1,2,0:T(8,128)} all-gather(f32[1,144,16]{1,2,0:T(8,128)S(1)} %get-tuple-element.282), channel_id=44, replica_groups=mesh['row'=16,'col'=2] {'row'}, dimensions={0}, use_global_device_ids=true | all-gather | bytes 156672 | tf_op jit(solution)/shard_map/all_gather | solution.py:23
  800.7 20.9 %all-gather.111 = f32[16,144,16]{1,2,0:T(8,128)} all-gather(f32[1,144,16]{1,2,0:T(8,128)S(1)} %get-tuple-element.281), channel_id=45, replica_groups=mesh['row'=16,'col'=2] {'row'}, dimensions={0}, use_global_device_ids=true | all-gather | bytes 156672 | tf_op jit(solution)/shard_map/all_gather | solution.py:23
  823.2 19.5 %all-gather.112 = f32[16,144,16]{1,2,0:T(8,128)} all-gather(f32[1,144,16]{1,2,0:T(8,128)S(1)} %get-tuple-element.280), channel_id=46, replica_groups=mesh['row'=16,'col'=2] {'row'}, dimensions={0}, use_global_device_ids=true | all-gather | bytes 156672 | tf_op jit(solution)/shard_map/all_gather | solution.py:23
  859.9 20.9 %all-gather.29 = bf16[32,192,16]{1,2,0:T(8,128)(2,1)} all-gather(bf16[2,192,16]{1,2,0:T(8,128)(2,1)S(1)} %get-tuple-element.223), channel_id=31, replica_groups=mesh['row'=16,'col'=2] {'row'}, dimensions={0}, use_global_device_ids=true | all-gather | bytes 208896 | tf_op jit(solution)/shard_map/all_gather | solution.py:23
  883.7 19.5 %all-gather.30 = bf16[32,192,16]{1,2,0:T(8,128)(2,1)} all-gather(bf16[2,192,16]{1,2,0:T(8,128)(2,1)S(1)} %get-tuple-element.217), channel_id=32, replica_groups=mesh['row'=16,'col'=2] {'row'}, dimensions={0}, use_global_device_ids=true | all-gather | bytes 208896 | tf_op jit(solution)/shard_map/all_gather | solution.py:23
  904.9 20.9 %all-gather.31 = bf16[32,192,16]{1,2,0:T(8,128)(2,1)} all-gather(bf16[2,192,16]{1,2,0:T(8,128)(2,1)S(1)} %get-tuple-element.218), channel_id=33, replica_groups=mesh['row'=16,'col'=2] {'row'}, dimensions={0}, use_global_device_ids=true | all-gather | bytes 208896 | tf_op jit(solution)/shard_map/all_gather | solution.py:23
  927.3 19.5 %all-gather.32 = bf16[32,192,16]{1,2,0:T(8,128)(2,1)} all-gather(bf16[2,192,16]{1,2,0:T(8,128)(2,1)S(1)} %get-tuple-element.219), channel_id=34, replica_groups=mesh['row'=16,'col'=2] {'row'}, dimensions={0}, use_global_device_ids=true | all-gather | bytes 208896 | tf_op jit(solution)/shard_map/all_gather | solution.py:23
  948.5 20.9 %all-gather.33 = bf16[32,192,16]{1,2,0:T(8,128)(2,1)} all-gather(bf16[2,192,16]{1,2,0:T(8,128)(2,1)S(1)} %get-tuple-element.220), channel_id=35, replica_groups=mesh['row'=16,'col'=2] {'row'}, dimensions={0}, use_global_device_ids=true | all-gather | bytes 208896 | tf_op jit(solution)/shard_map/all_gather | solution.py:23
  971.0 19.5 %all-gather.34 = bf16[32,192,16]{1,2,0:T(8,128)(2,1)} all-gather(bf16[2,192,16]{1,2,0:T(8,128)(2,1)S(1)} %get-tuple-element.221), channel_id=36, replica_groups=mesh['row'=16,'col'=2] {'row'}, dimensions={0}, use_global_device_ids=true | all-gather | bytes 208896 | tf_op jit(solution)/shard_map/all_gather | solution.py:23
  992.1 20.9 %all-gather.35 = bf16[32,192,16]{1,2,0:T(8,128)(2,1)} all-gather(bf16[2,192,16]{1,2,0:T(8,128)(2,1)S(1)} %get-tuple-element.222), channel_id=37, replica_groups=mesh['row'=16,'col'=2] {'row'}, dimensions={0}, use_global_device_ids=true | all-gather | bytes 208896 | tf_op jit(solution)/shard_map/all_gather | solution.py:23
  1014.6 19.5 %all-gather.36 = bf16[32,192,16]{1,2,0:T(8,128)(2,1)} all-gather(bf16[2,192,16]{1,2,0:T(8,128)(2,1)S(1)} %get-tuple-element.216), channel_id=38, replica_groups=mesh['row'=16,'col'=2] {'row'}, dimensions={0}, use_global_device_ids=true | all-gather | bytes 208896 | tf_op jit(solution)/shard_map/all_gather | solution.py:23
  1065.1 21.4 %all-gather.115 = f32[16,288,16]{1,2,0:T(8,128)} all-gather(f32[1,288,16]{1,2,0:T(8,128)S(1)} %get-tuple-element.215), channel_id=50, replica_groups=mesh['row'=16,'col'=2] {'row'}, dimensions={0}, use_global_device_ids=true | all-gather | bytes 313344 | tf_op jit(solution)/shard_map/all_gather | solution.py:23
  1089.4 20.1 %all-gather.116 = f32[16,288,16]{1,2,0:T(8,128)} all-gather(f32[1,288,16]{1,2,0:T(8,128)} %get-tuple-element.214), channel_id=51, replica_groups=mesh['row'=16,'col'=2] {'row'}, dimensions={0}, use_global_device_ids=true | all-gather | bytes 313344 | tf_op jit(solution)/shard_map/all_gather | solution.py:23
  1112.6 21.5 %all-gather.117 = f32[16,288,16]{1,2,0:T(8,128)} all-gather(f32[1,288,16]{1,2,0:T(8,128)} %get-tuple-element.213), channel_id=52, replica_groups=mesh['row'=16,'col'=2] {'row'}, dimensions={0}, use_global_device_ids=true | all-gather | bytes 313344 | tf_op jit(solution)/shard_map/all_gather | solution.py:23
  1137.1 20.1 %all-gather.118 = f32[16,288,16]{1,2,0:T(8,128)} all-gather(f32[1,288,16]{1,2,0:T(8,128)} %get-tuple-element.212), channel_id=53, replica_groups=mesh['row'=16,'col'=2] {'row'}, dimensions={0}, use_global_device_ids=true | all-gather | bytes 313344 | tf_op jit(solution)/shard_map/all_gather | solution.py:23
  1160.2 21.5 %all-gather.119 = f32[16,288,16]{1,2,0:T(8,128)} all-gather(f32[1,288,16]{1,2,0:T(8,128)} %get-tuple-element.211), channel_id=54, replica_groups=mesh['row'=16,'col'=2] {'row'}, dimensions={0}, use_global_device_ids=true | all-gather | bytes 313344 | tf_op jit(solution)/shard_map/all_gather | solution.py:23
  1184.7 20.1 %all-gather.120 = f32[16,288,16]{1,2,0:T(8,128)} all-gather(f32[1,288,16]{1,2,0:T(8,128)} %get-tuple-element.210), channel_id=55, replica_groups=mesh['row'=16,'col'=2] {'row'}, dimensions={0}, use_global_device_ids=true | all-gather | bytes 313344 | tf_op jit(solution)/shard_map/all_gather | solution.py:23
  1207.8 21.5 %all-gather.121 = f32[16,288,16]{1,2,0:T(8,128)} all-gather(f32[1,288,16]{1,2,0:T(8,128)} %get-tuple-element.209), channel_id=56, replica_groups=mesh['row'=16,'col'=2] {'row'}, dimensions={0}, use_global_device_ids=true | all-gather | bytes 313344 | tf_op jit(solution)/shard_map/all_gather | solution.py:23
  1232.3 20.1 %all-gather.122 = f32[16,288,16]{1,2,0:T(8,128)} all-gather(f32[1,288,16]{1,2,0:T(8,128)} %get-tuple-element.208), channel_id=57, replica_groups=mesh['row'=16,'col'=2] {'row'}, dimensions={0}, use_global_device_ids=true | all-gather | bytes 313344 | tf_op jit(solution)/shard_map/all_gather | solution.py:23
  1295.3 20.9 %all-gather.123 = f32[16,144,16]{1,2,0:T(8,128)} all-gather(f32[1,144,16]{1,2,0:T(8,128)S(1)} %get-tuple-element.275), channel_id=68, replica_groups=mesh['row'=16,'col'=2] {'row'}, dimensions={0}, use_global_device_ids=true | all-gather | bytes 156672 | tf_op jit(solution)/shard_map/all_gather | solution.py:23
  1317.8 19.7 %all-gather.124 = f32[16,144,16]{1,2,0:T(8,128)} all-gather(f32[1,144,16]{1,2,0:T(8,128)S(1)} %get-tuple-element.274), channel_id=69, replica_groups=mesh['row'=16,'col'=2] {'row'}, dimensions={0}, use_global_device_ids=true | all-gather | bytes 156672 | tf_op jit(solution)/shard_map/all_gather | solution.py:23
  1339.1 20.9 %all-gather.125 = f32[16,144,16]{1,2,0:T(8,128)} all-gather(f32[1,144,16]{1,2,0:T(8,128)S(1)} %get-tuple-element.273), channel_id=70, replica_groups=mesh['row'=16,'col'=2] {'row'}, dimensions={0}, use_global_device_ids=true | all-gather | bytes 156672 | tf_op jit(solution)/shard_map/all_gather | solution.py:23
  1361.5 19.5 %all-gather.126 = f32[16,144,16]{1,2,0:T(8,128)} all-gather(f32[1,144,16]{1,2,0:T(8,128)S(1)} %get-tuple-element.272), channel_id=71, replica_groups=mesh['row'=16,'col'=2] {'row'}, dimensions={0}, use_global_device_ids=true | all-gather | bytes 156672 | tf_op jit(solution)/shard_map/all_gather | solution.py:23
  1382.6 20.9 %all-gather.127 = f32[16,144,16]{1,2,0:T(8,128)} all-gather(f32[1,144,16]{1,2,0:T(8,128)S(1)} %get-tuple-element.271), channel_id=72, replica_groups=mesh['row'=16,'col'=2] {'row'}, dimensions={0}, use_global_device_ids=true | all-gather | bytes 156672 | tf_op jit(solution)/shard_map/all_gather | solution.py:23
  1405.1 19.5 %all-gather.128 = f32[16,144,16]{1,2,0:T(8,128)} all-gather(f32[1,144,16]{1,2,0:T(8,128)S(1)} %get-tuple-element.270), channel_id=73, replica_groups=mesh['row'=16,'col'=2] {'row'}, dimensions={0}, use_global_device_ids=true | all-gather | bytes 156672 | tf_op jit(solution)/shard_map/all_gather | solution.py:23
  1426.2 20.9 %all-gather.129 = f32[16,144,16]{1,2,0:T(8,128)} all-gather(f32[1,144,16]{1,2,0:T(8,128)S(1)} %get-tuple-element.269), channel_id=74, replica_groups=mesh['row'=16,'col'=2] {'row'}, dimensions={0}, use_global_device_ids=true | all-gather | bytes 156672 | tf_op jit(solution)/shard_map/all_gather | solution.py:23
  1448.6 19.5 %all-gather.130 = f32[16,144,16]{1,2,0:T(8,128)} all-gather(f32[1,144,16]{1,2,0:T(8,128)S(1)} %get-tuple-element.268), channel_id=75, replica_groups=mesh['row'=16,'col'=2] {'row'}, dimensions={0}, use_global_device_ids=true | all-gather | bytes 156672 | tf_op jit(solution)/shard_map/all_gather | solution.py:23
  1485.3 20.9 %all-gather.58 = bf16[32,192,16]{1,2,0:T(8,128)(2,1)} all-gather(bf16[2,192,16]{1,2,0:T(8,128)(2,1)S(1)} %get-tuple-element.207), channel_id=60, replica_groups=mesh['row'=16,'col'=2] {'row'}, dimensions={0}, use_global_device_ids=true | all-gather | bytes 208896 | tf_op jit(solution)/shard_map/all_gather | solution.py:23
  1509.1 19.5 %all-gather.59 = bf16[32,192,16]{1,2,0:T(8,128)(2,1)} all-gather(bf16[2,192,16]{1,2,0:T(8,128)(2,1)S(1)} %get-tuple-element.201), channel_id=61, replica_groups=mesh['row'=16,'col'=2] {'row'}, dimensions={0}, use_global_device_ids=true | all-gather | bytes 208896 | tf_op jit(solution)/shard_map/all_gather | solution.py:23
  1530.3 20.9 %all-gather.60 = bf16[32,192,16]{1,2,0:T(8,128)(2,1)} all-gather(bf16[2,192,16]{1,2,0:T(8,128)(2,1)S(1)} %get-tuple-element.202), channel_id=62, replica_groups=mesh['row'=16,'col'=2] {'row'}, dimensions={0}, use_global_device_ids=true | all-gather | bytes 208896 | tf_op jit(solution)/shard_map/all_gather | solution.py:23
  1552.8 19.5 %all-gather.61 = bf16[32,192,16]{1,2,0:T(8,128)(2,1)} all-gather(bf16[2,192,16]{1,2,0:T(8,128)(2,1)S(1)} %get-tuple-element.203), channel_id=63, replica_groups=mesh['row'=16,'col'=2] {'row'}, dimensions={0}, use_global_device_ids=true | all-gather | bytes 208896 | tf_op jit(solution)/shard_map/all_gather | solution.py:23
  1573.9 20.9 %all-gather.62 = bf16[32,192,16]{1,2,0:T(8,128)(2,1)} all-gather(bf16[2,192,16]{1,2,0:T(8,128)(2,1)S(1)} %get-tuple-element.204), channel_id=64, replica_groups=mesh['row'=16,'col'=2] {'row'}, dimensions={0}, use_global_device_ids=true | all-gather | bytes 208896 | tf_op jit(solution)/shard_map/all_gather | solution.py:23
  1596.4 19.5 %all-gather.63 = bf16[32,192,16]{1,2,0:T(8,128)(2,1)} all-gather(bf16[2,192,16]{1,2,0:T(8,128)(2,1)S(1)} %get-tuple-element.205), channel_id=65, replica_groups=mesh['row'=16,'col'=2] {'row'}, dimensions={0}, use_global_device_ids=true | all-gather | bytes 208896 | tf_op jit(solution)/shard_map/all_gather | solution.py:23
  1617.5 20.9 %all-gather.64 = bf16[32,192,16]{1,2,0:T(8,128)(2,1)} all-gather(bf16[2,192,16]{1,2,0:T(8,128)(2,1)S(1)} %get-tuple-element.206), channel_id=66, replica_groups=mesh['row'=16,'col'=2] {'row'}, dimensions={0}, use_global_device_ids=true | all-gather | bytes 208896 | tf_op jit(solution)/shard_map/all_gather | solution.py:23
  1640.0 19.7 %all-gather.65 = bf16[32,192,16]{1,2,0:T(8,128)(2,1)} all-gather(bf16[2,192,16]{1,2,0:T(8,128)(2,1)S(1)} %get-tuple-element.200), channel_id=67, replica_groups=mesh['row'=16,'col'=2] {'row'}, dimensions={0}, use_global_device_ids=true | all-gather | bytes 208896 | tf_op jit(solution)/shard_map/all_gather | solution.py:23
  1689.2 21.2 %all-gather.133 = f32[16,288,16]{1,2,0:T(8,128)} all-gather(f32[1,288,16]{1,2,0:T(8,128)S(1)} %get-tuple-element.199), channel_id=79, replica_groups=mesh['row'=16,'col'=2] {'row'}, dimensions={0}, use_global_device_ids=true | all-gather | bytes 313344 | tf_op jit(solution)/shard_map/all_gather | solution.py:23
  1713.4 20.3 %all-gather.134 = f32[16,288,16]{1,2,0:T(8,128)} all-gather(f32[1,288,16]{1,2,0:T(8,128)} %get-tuple-element.198), channel_id=80, replica_groups=mesh['row'=16,'col'=2] {'row'}, dimensions={0}, use_global_device_ids=true | all-gather | bytes 313344 | tf_op jit(solution)/shard_map/all_gather | solution.py:23
  1736.6 21.5 %all-gather.135 = f32[16,288,16]{1,2,0:T(8,128)} all-gather(f32[1,288,16]{1,2,0:T(8,128)} %get-tuple-element.197), channel_id=81, replica_groups=mesh['row'=16,'col'=2] {'row'}, dimensions={0}, use_global_device_ids=true | all-gather | bytes 313344 | tf_op jit(solution)/shard_map/all_gather | solution.py:23
  1761.1 20.1 %all-gather.136 = f32[16,288,16]{1,2,0:T(8,128)} all-gather(f32[1,288,16]{1,2,0:T(8,128)} %get-tuple-element.196), channel_id=82, replica_groups=mesh['row'=16,'col'=2] {'row'}, dimensions={0}, use_global_device_ids=true | all-gather | bytes 313344 | tf_op jit(solution)/shard_map/all_gather | solution.py:23
  1784.2 21.5 %all-gather.137 = f32[16,288,16]{1,2,0:T(8,128)} all-gather(f32[1,288,16]{1,2,0:T(8,128)} %get-tuple-element.195), channel_id=83, replica_groups=mesh['row'=16,'col'=2] {'row'}, dimensions={0}, use_global_device_ids=true | all-gather | bytes 313344 | tf_op jit(solution)/shard_map/all_gather | solution.py:23
  1808.7 20.1 %all-gather.138 = f32[16,288,16]{1,2,0:T(8,128)} all-gather(f32[1,288,16]{1,2,0:T(8,128)} %get-tuple-element.194), channel_id=84, replica_groups=mesh['row'=16,'col'=2] {'row'}, dimensions={0}, use_global_device_ids=true | all-gather | bytes 313344 | tf_op jit(solution)/shard_map/all_gather | solution.py:23
  1831.8 21.3 %all-gather.139 = f32[16,288,16]{1,2,0:T(8,128)} all-gather(f32[1,288,16]{1,2,0:T(8,128)S(1)} %get-tuple-element.193), channel_id=85, replica_groups=mesh['row'=16,'col'=2] {'row'}, dimensions={0}, use_global_device_ids=true | all-gather | bytes 313344 | tf_op jit(solution)/shard_map/all_gather | solution.py:23
  1854.7 19.9 %all-gather.140 = f32[16,288,16]{1,2,0:T(8,128)} all-gather(f32[1,288,16]{1,2,0:T(8,128)S(1)} %get-tuple-element.192), channel_id=86, replica_groups=mesh['row'=16,'col'=2] {'row'}, dimensions={0}, use_global_device_ids=true | all-gather | bytes 313344 | tf_op jit(solution)/shard_map/all_gather | solution.py:23
  (624 shorter events, 574.0 us)
Async XLA Ops:
  0.6 651.8 %copy-start = (f32[2112,384]{1,0:T(8,128)S(1)}, f32[2112,384]{1,0:T(8,128)}, u32[]{:S(2)}) copy-start(f32[2112,384]{1,0:T(8,128)} %param.28) | copy-start | bytes 9732100
  2.5 9.4 copy-start.77
  2.5 9.4 copy-start.78
  2.5 9.4 copy-start.79
  2.5 9.3 copy-start.82
  2.5 9.3 copy-start.84
  3.0 183.0 %copy-start.22 = (f32[8,384]{1,0:T(8,128)S(1)}, f32[8,384]{1,0:T(8,128)}, u32[]{:S(2)}) copy-start(f32[8,384]{1,0:T(8,128)} %param.20) | copy-start | bytes 36868
  5.9 6.0 copy-start.85
  5.9 6.0 copy-start.86
  5.9 6.0 copy-start.87
  185.0 8.2 copy-start.90
  186.0 177.7 %copy-start.94 = (s32[8]{0:T(128)S(1)}, s32[8]{0:T(128)}, u32[]{:S(2)}) copy-start(s32[8]{0:T(128)} %param.24) | copy-start | bytes 100
  410.8 25.0 %copy-start.76 = (f32[8]{0:T(128)S(1)}, f32[8]{0:T(128)}, u32[]{:S(2)}) copy-start(f32[8]{0:T(128)} %copy-done.75) | copy-start | bytes 100
  413.7 9.8 copy-start.25
  415.6 118.2 %copy-start.20 = (f32[12,16]{1,0:T(8,128)}, f32[12,16]{1,0:T(8,128)S(1)}, u32[]{:S(2)}) copy-start(f32[12,16]{1,0:T(8,128)S(1)} %get-tuple-element.414) | copy-start | bytes 2308
  415.8 7.7 copy-start.8
  533.8 111.2 %copy-start.9 = (bf16[12,16,128]{2,1,0:T(8,128)(2,1)S(1)}, bf16[12,16,128]{2,1,0:T(8,128)(2,1)}, u32[]{:S(2)}) copy-start(bf16[12,16,128]{2,1,0:T(8,128)(2,1)} %copy-done.8) | copy-start | bytes 147460
  645.9 10.5 copy-start.72
  656.2 4.2 copy-start.89
  656.5 9.0 copy-start.93
  657.6 5.5 copy-start.65
  657.6 7.9 copy-start.64
  658.4 7.1 copy-start.63
  659.4 6.1 copy-start.48
  660.4 5.0 copy-start.31
  660.4 5.0 copy-start.26
  660.4 5.0 copy-start.29
  669.9 175.4 %copy-start.60 = (f32[1,48,8]{1,2,0:T(8,128)S(1)}, f32[1,48,8]{1,2,0:T(8,128)}, u32[]{:S(2)}) copy-start(f32[1,48,8]{1,2,0:T(8,128)} %get-tuple-element.247) | copy-start | bytes 4612
  669.9 175.4 %copy-start.61 = (f32[1,48,8]{1,2,0:T(8,128)S(1)}, f32[1,48,8]{1,2,0:T(8,128)}, u32[]{:S(2)}) copy-start(f32[1,48,8]{1,2,0:T(8,128)} %get-tuple-element.249) | copy-start | bytes 4612
  692.4 153.0 %copy-start.62 = (f32[1,48,8]{1,2,0:T(8,128)S(1)}, f32[1,48,8]{1,2,0:T(8,128)}, u32[]{:S(2)}) copy-start(f32[1,48,8]{1,2,0:T(8,128)} %get-tuple-element.251) | copy-start | bytes 4612
  1040.6 18.5 copy-start.21
  1134.1 131.2 %copy-start.14 = (f32[12,8]{1,0:T(8,128)S(1)}, f32[12,8]{1,0:T(8,128)}, u32[]{:S(2)}) copy-start(f32[12,8]{1,0:T(8,128)} %copy-done.13) | copy-start | bytes 1156
  1134.1 131.2 %copy-start.16 = (f32[12,8]{1,0:T(8,128)S(1)}, f32[12,8]{1,0:T(8,128)}, u32[]{:S(2)}) copy-start(f32[12,8]{1,0:T(8,128)} %copy-done.15) | copy-start | bytes 1156
  1158.9 110.1 %copy-start.27 = (f32[1,8]{1,0:T(1,128)S(1)}, f32[1,8]{1,0:T(1,128)}, u32[]{:S(2)}) copy-start(f32[1,8]{1,0:T(1,128)} %copy-done.26) | copy-start | bytes 100
  1279.0 11.0 copy-start.30
  1279.0 11.0 copy-start.49
  1279.0 11.0 copy-start.57
  1279.0 11.2 copy-start.28
  1279.0 11.2 copy-start.39
  1279.0 11.2 copy-start.41
  1279.9 4.9 copy-start.73
  1284.6 194.2 %copy-start.88 = (f32[8]{0:T(128)}, f32[8]{0:T(128)S(1)}, u32[]{:S(2)}) copy-start(f32[8]{0:T(128)S(1)} %broadcast_multiply_fusion.7) | copy-start | bytes 100
  1284.8 5.4 copy-start.91
  1285.7 4.3 copy-start.66
  1290.3 5.1 copy-start.50
  1317.8 161.0 %copy-start.92 = (f32[8]{0:T(128)S(1)}, f32[8]{0:T(128)}, u32[]{:S(2)}) copy-start(f32[8]{0:T(128)} %copy-done.91) | copy-start | bytes 100
  1666.2 17.9 copy-start.18
  1682.4 203.7 %copy-start.10 = (f32[12,8]{1,0:T(8,128)}, f32[12,8]{1,0:T(8,128)S(1)}, u32[]{:S(2)}) copy-start(f32[12,8]{1,0:T(8,128)S(1)} %get-tuple-element.344) | copy-start | bytes 1156
  1682.4 203.7 %copy-start.11 = (f32[12,8]{1,0:T(8,128)}, f32[12,8]{1,0:T(8,128)S(1)}, u32[]{:S(2)}) copy-start(f32[12,8]{1,0:T(8,128)S(1)} %get-tuple-element.345) | copy-start | bytes 1156
  1682.4 203.7 %copy-start.12 = (f32[12,8]{1,0:T(8,128)}, f32[12,8]{1,0:T(8,128)S(1)}, u32[]{:S(2)}) copy-start(f32[12,8]{1,0:T(8,128)S(1)} %get-tuple-element.346) | copy-start | bytes 1156
  1713.4 164.5 %copy-start.19 = (f32[12,16]{1,0:T(8,128)S(1)}, f32[12,16]{1,0:T(8,128)}, u32[]{:S(2)}) copy-start(f32[12,16]{1,0:T(8,128)} %copy-done.18) | copy-start | bytes 2308
  1782.9 103.6 %copy-start.33 = (f32[1,8]{1,0:T(1,128)S(1)}, f32[1,8]{1,0:T(1,128)}, u32[]{:S(2)}) copy-start(f32[1,8]{1,0:T(1,128)} %copy-done.32) | copy-start | bytes 100
  1782.9 103.6 %copy-start.35 = (f32[1,8]{1,0:T(1,128)S(1)}, f32[1,8]{1,0:T(1,128)}, u32[]{:S(2)}) copy-start(f32[1,8]{1,0:T(1,128)} %copy-done.34) | copy-start | bytes 100
  1782.9 103.6 %copy-start.37 = (f32[1,8]{1,0:T(1,128)S(1)}, f32[1,8]{1,0:T(1,128)}, u32[]{:S(2)}) copy-start(f32[1,8]{1,0:T(1,128)} %copy-done.36) | copy-start | bytes 100
  1886.4 12.6 copy-start.74
  1886.4 12.8 copy-start.51
  1886.4 12.8 copy-start.53
  1886.4 12.8 copy-start.55
  1886.4 12.8 copy-start.69
  1886.5 12.7 copy-start.67
  1886.5 12.7 copy-start.43
  1886.5 12.7 copy-start.45
  1886.5 12.7 copy-start.47
  1886.6 12.7 copy-start.71
  (31 other events, 73.3 us)
